TPU v7x, 256 devices: a whole 4x4x8 slice. The times are simulated.
256 devices in a mesh: shard: 64 (over z, x, core), model: 4 (over y).
Axes of the slice: x: 4, y: 4, z: 8, core: 2. Of those that a mesh axis runs over, the one named last changes fastest.
Arguments:
- grad_stack: float32 [512, 128, 2048], P(None, 'shard', 'model'), may hold values from -6 to 6
- moment_stack: float32 [512, 128, 2048], P(None, 'shard', 'model'), may hold values from -6 to 6
- weight_stack: float32 [512, 128, 2048], P(None, 'shard', 'model'), may hold values from -0.1875 to 0.1875
Outputs:
- new_weights: float32 [512, 128, 2048], P(None, 'shard', 'model')
- new_momentum: float32 [512, 128, 2048], P(None, 'shard', 'model')
All inputs are finite; a program needn't handle non-finite values.
Results may differ from a plain program's by a relative error of at most 0.00021.
Values sent between devices are 32-bit elements; how exact they have to be, the bound alone decides.
A program may use at most 64 MiB of HBM per device.

v0:
```python
import jax
import jax.numpy as jnp
from jax import lax
from jax.sharding import PartitionSpec as P

hold_rate = 0.95
learn_rate = 1.0
decay_rate = 0.1
HIGH = lax.Precision.HIGHEST


def mul(a, b):
    return jnp.einsum("mij,mjk->mik", a, b, precision=HIGH)


def chain(gram, steps):
    eye = jnp.eye(gram.shape[-1], dtype=gram.dtype)
    total = None
    for step in range(steps):
        factor = 3.4445 * eye - 4.775 * gram + 2.0315 * mul(gram, gram)
        total = factor if total is None else mul(factor, total)
        if step < steps - 1:
            gram = mul(mul(factor, gram), factor)
    return total


def summed_gram(rows):
    part = jnp.einsum("mik,mjk->mij", rows, rows, precision=HIGH)
    parts = lax.all_to_all(part, "model", split_axis=0, concat_axis=0, tiled=True)
    return parts.reshape(4, -1, *parts.shape[1:]).sum(axis=0)


def on_device(grad_stack, moment_stack, weight_stack):
    new_momentum = hold_rate * moment_stack + grad_stack
    rows = lax.all_to_all(new_momentum, "shard", split_axis=0, concat_axis=1, tiled=True)
    gram = summed_gram(rows)
    scale = lax.rsqrt(jnp.trace(gram, axis1=1, axis2=2)[:, None, None] + 1e-06)
    first = chain(gram * scale * scale, 2) * scale
    rows = mul(lax.all_gather(first, "model", axis=0, tiled=True), rows)
    second = chain(summed_gram(rows), 3)
    rows = mul(lax.all_gather(second, "model", axis=0, tiled=True), rows)
    back = lax.all_to_all(rows, "shard", split_axis=1, concat_axis=0, tiled=True)
    new_weights = (1.0 - learn_rate * decay_rate) * weight_stack - learn_rate * back
    return (new_weights, new_momentum)


def solution(mesh):
    spec = P(None, "shard", "model")
    return jax.shard_map(
        on_device, mesh=mesh, in_specs=(spec,) * 3, out_specs=(spec,) * 2, check_vma=False
    )
```

profile of v0, /device:TPU:2, one launch (start us, length us, event | category | flops | bytes accessed | tf_op | source)
XLA Modules:
  0.0 198.5 jit_solution(3235271127646908158)
XLA Ops:
  0.6 3.7 %multiply_add_fusion = f32[512,2,512]{2,1,0:T(2,128)S(1)} fusion(f32[512,2,512]{2,1,0:T(2,128)} %param.3, f32[512,2,512]{2,1,0:T(2,128)} %param.4), kind=kLoop, calls=%fused_computation.2 | loop fusion | flops 1048576 | bytes 6291456 | tf_op jit(solution)/shard_map/add | solution.py:34
  4.3 63.1 %all_to_all.46 = f32[512,2,512]{2,1,0:T(2,128)S(1)} all-to-all(f32[512,2,512]{2,1,0:T(2,128)S(1)} %multiply_add_fusion), channel_id=1, replica_groups=mesh['shard'=64,'model'=4] {'shard'}, dimensions={0} | all-to-all | bytes 4194304 | tf_op jit(solution)/shard_map/all_to_all | solution.py:35
  67.4 2.1 %copy.11 = f32[64,8,2,512]{3,2,0,1:T(2,128)} copy(f32[64,8,2,512]{3,2,1,0:T(2,128)S(1)} %bitcast.46) | data formatting | bytes 4194304 | tf_op jit(solution)/shard_map/all_to_all | solution.py:35
  69.4 2.7 %all_to_all.35 = f32[8,128,512]{2,1,0:T(8,128)S(1)} reshape(f32[8,64,2,512]{3,2,1,0:T(2,128)} %bitcast.44) | data formatting | bytes 4194304 | tf_op jit(solution)/shard_map/all_to_all | solution.py:35
  72.1 2.9 %fusion.8 = f32[8,128,128]{2,1,0:T(8,128)} fusion(f32[8,128,512]{2,1,0:T(8,128)S(1)} %all_to_all.35), kind=kOutput, calls=%fused_computation.22 | convolution fusion | flops 805306368 | bytes 2621440 | tf_op jit(solution)/shard_map/mik,mjk->mij/dot_general | solution.py:28
  75.0 4.5 %all-to-all-start.1 = ((f32[8,128,128]{2,1,0:T(8,128)}), f32[8,128,128]{2,1,0:T(8,128)S(1)}, u32[]{:S(2)}, u32[]{:S(2)}) async-start(f32[8,128,128]{2,1,0:T(8,128)} %fusion.8), calls=%async_computation.1 | async-start | bytes 1048576 | tf_op jit(solution)/shard_map/all_to_all | solution.py:29
  79.5 8.0 %all-to-all-done.1 = f32[8,128,128]{2,1,0:T(8,128)S(1)} async-done(((f32[8,128,128]{2,1,0:T(8,128)}), f32[8,128,128]{2,1,0:T(8,128)S(1)}, u32[]{:S(2)}, u32[]{:S(2)}) %all-to-all-start.1) | async-done | bytes 524320 | tf_op jit(solution)/shard_map/all_to_all | solution.py:29
  87.6 0.1 select_reduce_fusion
  87.7 0.4 fusion.4
  88.1 0.3 fusion.5
  88.4 0.3 fusion.9
  88.7 0.3 fusion.3
  89.0 0.3 convolution_multiply_fusion.3
  89.2 12.8 %all_gather.6 = f32[8,128,128]{2,1,0:T(8,128)S(1)} all-gather(f32[2,128,128]{2,1,0:T(8,128)S(1)} %convolution_multiply_fusion.3), channel_id=1, replica_groups=mesh['shard'=64,'model'=4] {'model'}, dimensions={0}, use_global_device_ids=true | all-gather | bytes 655360 | tf_op jit(solution)/shard_map/all_gather | solution.py:39
  102.0 1.8 fusion.10
  103.9 2.1 %fusion.11 = f32[8,128,128]{2,1,0:T(8,128)S(1)} fusion(f32[8,128,512]{2,1,0:T(8,128)S(1)} %fusion.10), kind=kOutput, calls=%fused_computation.25 | convolution fusion | flops 805306368 | bytes 2621440 | tf_op jit(solution)/shard_map/mik,mjk->mij/dot_general | solution.py:28
  106.0 11.3 %all_to_all.47 = f32[8,128,128]{2,1,0:T(8,128)S(1)} all-to-all(f32[8,128,128]{2,1,0:T(8,128)S(1)} %fusion.11), channel_id=1, replica_groups=mesh['shard'=64,'model'=4] {'model'}, dimensions={0} | all-to-all | bytes 1048576 | tf_op jit(solution)/shard_map/all_to_all | solution.py:29
  117.4 0.3 fusion.2
  117.6 0.3 fusion.12
  117.9 0.3 fusion.13
  118.2 0.3 fusion.1
  118.5 0.3 fusion.16
  118.7 0.3 fusion.14
  119.0 0.3 fusion.15
  119.3 0.3 fusion
  119.6 0.3 fusion.17
  119.8 12.8 %all_gather.7 = f32[8,128,128]{2,1,0:T(8,128)S(1)} all-gather(f32[2,128,128]{2,1,0:T(8,128)S(1)} %fusion.17), channel_id=1, replica_groups=mesh['shard'=64,'model'=4] {'model'}, dimensions={0}, use_global_device_ids=true | all-gather | bytes 655360 | tf_op jit(solution)/shard_map/all_gather | solution.py:41
  132.6 1.8 fusion.18
  134.5 1.2 copy.8
  135.7 57.6 %all_to_all.48 = f32[8,128,512]{2,0,1:T(8,128)S(1)} all-to-all(f32[8,128,512]{2,0,1:T(8,128)S(1)} %copy.8), channel_id=1, replica_groups=mesh['shard'=64,'model'=4] {'shard'}, dimensions={1} | all-to-all | bytes 4194304 | tf_op jit(solution)/shard_map/all_to_all | solution.py:42
  193.3 1.9 copy.9
  195.3 3.3 %bitcast_subtract_fusion = f32[512,2,512]{2,1,0:T(2,128)} fusion(f32[64,8,2,512]{3,2,1,0:T(2,128)S(1)} %copy.9, f32[512,2,512]{2,1,0:T(2,128)S(1)} %copy-done.3), kind=kLoop, calls=%fused_computation | loop fusion | flops 1048576 | bytes 6291456 | tf_op jit(solution)/shard_map/sub | solution.py:43
  (13 shorter events, 0.1 us)
Async XLA Ops:
  4.3 63.1 %copy-start.2 = (f32[512,2,512]{2,1,0:T(2,128)}, f32[512,2,512]{2,1,0:T(2,128)S(1)}, u32[]{:S(2)}) copy-start(f32[512,2,512]{2,1,0:T(2,128)S(1)} %multiply_add_fusion) | copy-start | bytes 6291460
  75.0 12.5 %all-to-all-start.1 = ((f32[8,128,128]{2,1,0:T(8,128)}), f32[8,128,128]{2,1,0:T(8,128)S(1)}, u32[]{:S(2)}, u32[]{:S(2)}) async-start(f32[8,128,128]{2,1,0:T(8,128)} %fusion.8), calls=%async_computation.1 | async-start | bytes 1048576 | tf_op jit(solution)/shard_map/all_to_all | solution.py:29
  103.9 2.1 %copy-start = (f32[8,128,512]{2,1,0:T(8,128)}, f32[8,128,512]{2,1,0:T(8,128)S(1)}, u32[]{:S(2)}) copy-start(f32[8,128,512]{2,1,0:T(8,128)S(1)} %fusion.10) | copy-start | bytes 6291460
  117.3 15.3 %copy-start.1 = (f32[8,128,512]{2,1,0:T(8,128)S(1)}, f32[8,128,512]{2,1,0:T(8,128)}, u32[]{:S(2)}) copy-start(f32[8,128,512]{2,1,0:T(8,128)} %copy-done) | copy-start | bytes 6291460
  193.3 1.9 copy-start.3
where the time goes:
time: 199 us
  blocking collectives  158 us (79%)
  matrix products  12.5 us (6%)
  waiting for transfers between devices  8.05 us (4%)
  local copies, waits for them, and re-layouts  7.95 us (4%)
  other arithmetic  7.12 us (4%)
  starting transfers between devices  4.46 us (2%)
    all_to_all x1, blocking collectives, on_device(): lax.all_to_all(new_momentum, 'shard', split_axis=0, concat_axis=1, tiled=...  63.1 us
    all_to_all x1, blocking collectives, on_device(): lax.all_to_all(rows, 'shard', split_axis=1, concat_axis=0, tiled=True)  57.6 us
    all_gather x1, blocking collectives, on_device(): rows = mul(lax.all_gather(first, 'model', axis=0, tiled=True), rows)  12.8 us
    all_gather x1, blocking collectives, on_device(): rows = mul(lax.all_gather(second, 'model', axis=0, tiled=True), rows)  12.8 us
    all_to_all x1, blocking collectives, summed_gram(): lax.all_to_all(part, 'model', split_axis=0, concat_axis=0, tiled=True)  11.3 us
    all_to_all x1, waiting for transfers between devices, summed_gram(): lax.all_to_all(part, 'model', split_axis=0, concat_axis=0, tiled=True)  8.05 us
    dot_general x16, matrix products, mul(): return jnp.einsum('mij,mjk->mik', a, b, precision=HIGH)  7.6 us
    dot_general x2, matrix products, summed_gram(): part = jnp.einsum('mik,mjk->mij', rows, rows, precision=HIGH)  4.93 us
  transfers between devices with their start and end apart: 1, of which 1 were waited for; matrix products, arithmetic and copies ran while one was open for 0% of the time, Pallas kernels for 0%

commit v1 on v0

--- a/solution.py
+++ b/solution.py
@@ -39,7 +39,10 @@
     rows = mul(lax.all_gather(first, "model", axis=0, tiled=True), rows)
     second = chain(summed_gram(rows), 3)
     rows = mul(lax.all_gather(second, "model", axis=0, tiled=True), rows)
-    back = lax.all_to_all(rows, "shard", split_axis=1, concat_axis=0, tiled=True)
+    back = jnp.concatenate(
+        lax.all_to_all(jnp.stack(jnp.split(rows, lax.axis_size("shard"), axis=1)), "shard", 0, 0),
+        axis=0,
+    )
     new_weights = (1.0 - learn_rate * decay_rate) * weight_stack - learn_rate * back
     return (new_weights, new_momentum)
 

time: 199 us -> 198 us (level)
  no operation moved by 1% of the time
where the time goes in v1:
time: 198 us; the launch traced here: 197 us
  blocking collectives  158 us (80%)
  matrix products  12.5 us (6%)
  waiting for transfers between devices  8.05 us (4%)
  other arithmetic  7.12 us (4%)
  local copies, waits for them, and re-layouts  6.18 us (3%)
  starting transfers between devices  4.46 us (2%)
    all_to_all x1, blocking collectives, on_device(): lax.all_to_all(new_momentum, 'shard', split_axis=0, concat_axis=1, tiled=...  63.1 us
    all_to_all x1, blocking collectives, on_device(): lax.all_to_all(jnp.stack(jnp.split(rows, lax.axis_size('shard'), axis=1))...  57.8 us
    all_gather x1, blocking collectives, on_device(): rows = mul(lax.all_gather(first, 'model', axis=0, tiled=True), rows)  12.8 us
    all_gather x1, blocking collectives, on_device(): rows = mul(lax.all_gather(second, 'model', axis=0, tiled=True), rows)  12.8 us
    all_to_all x1, blocking collectives, summed_gram(): lax.all_to_all(part, 'model', split_axis=0, concat_axis=0, tiled=True)  11.3 us
    all_to_all x1, waiting for transfers between devices, summed_gram(): lax.all_to_all(part, 'model', split_axis=0, concat_axis=0, tiled=True)  8.05 us
    dot_general x16, matrix products, mul(): return jnp.einsum('mij,mjk->mik', a, b, precision=HIGH)  7.6 us
    dot_general x2, matrix products, summed_gram(): part = jnp.einsum('mik,mjk->mij', rows, rows, precision=HIGH)  4.93 us
  transfers between devices with their start and end apart: 1, of which 1 were waited for; matrix products, arithmetic and copies ran while one was open for 0% of the time, Pallas kernels for 0%

profile of v1, /device:TPU:2, one launch (start us, length us, event | category | flops | bytes accessed | tf_op | source)
XLA Modules:
  0.0 197.3 jit_solution(1204164117297704647)
XLA Ops:
  0.6 3.7 %multiply_add_fusion = f32[512,2,512]{2,1,0:T(2,128)S(1)} fusion(f32[512,2,512]{2,1,0:T(2,128)} %param.3, f32[512,2,512]{2,1,0:T(2,128)} %param.4), kind=kLoop, calls=%fused_computation.2 | loop fusion | flops 1048576 | bytes 6291456 | tf_op jit(solution)/shard_map/add | solution.py:34
  4.3 0.0 copy-start.2
  4.3 63.1 %all_to_all.33 = f32[512,2,512]{2,1,0:T(2,128)S(1)} all-to-all(f32[512,2,512]{2,1,0:T(2,128)S(1)} %multiply_add_fusion), channel_id=1, replica_groups=mesh['shard'=64,'model'=4] {'shard'}, dimensions={0} | all-to-all | bytes 4194304 | tf_op jit(solution)/shard_map/all_to_all | solution.py:35
  67.4 2.1 %copy.8 = f32[64,8,2,512]{3,2,0,1:T(2,128)} copy(f32[64,8,2,512]{3,2,1,0:T(2,128)S(1)} %bitcast.298) | data formatting | bytes 4194304 | tf_op jit(solution)/shard_map/all_to_all | solution.py:35
  69.4 2.7 %all_to_all.25 = f32[8,128,512]{2,1,0:T(8,128)S(1)} reshape(f32[8,64,2,512]{3,2,1,0:T(2,128)} %bitcast.297) | data formatting | bytes 4194304 | tf_op jit(solution)/shard_map/all_to_all | solution.py:35
  72.1 2.9 %fusion.8 = f32[8,128,128]{2,1,0:T(8,128)} fusion(f32[8,128,512]{2,1,0:T(8,128)S(1)} %all_to_all.25), kind=kOutput, calls=%fused_computation.150 | convolution fusion | flops 805306368 | bytes 2621440 | tf_op jit(solution)/shard_map/mik,mjk->mij/dot_general | solution.py:28
  75.0 4.5 %all-to-all-start.1 = ((f32[8,128,128]{2,1,0:T(8,128)}), f32[8,128,128]{2,1,0:T(8,128)S(1)}, u32[]{:S(2)}, u32[]{:S(2)}) async-start(f32[8,128,128]{2,1,0:T(8,128)} %fusion.8), calls=%async_computation.1 | async-start | bytes 1048576 | tf_op jit(solution)/shard_map/all_to_all | solution.py:29
  79.5 8.0 %all-to-all-done.1 = f32[8,128,128]{2,1,0:T(8,128)S(1)} async-done(((f32[8,128,128]{2,1,0:T(8,128)}), f32[8,128,128]{2,1,0:T(8,128)S(1)}, u32[]{:S(2)}, u32[]{:S(2)}) %all-to-all-start.1) | async-done | bytes 524320 | tf_op jit(solution)/shard_map/all_to_all | solution.py:29
  87.6 0.1 select_reduce_fusion
  87.7 0.4 fusion.4
  88.1 0.3 fusion.5
  88.4 0.3 fusion.9
  88.7 0.3 fusion.3
  89.0 0.3 convolution_multiply_fusion.3
  89.2 12.8 %all_gather.6 = f32[8,128,128]{2,1,0:T(8,128)S(1)} all-gather(f32[2,128,128]{2,1,0:T(8,128)S(1)} %convolution_multiply_fusion.3), channel_id=1, replica_groups=mesh['shard'=64,'model'=4] {'model'}, dimensions={0}, use_global_device_ids=true | all-gather | bytes 655360 | tf_op jit(solution)/shard_map/all_gather | solution.py:39
  102.0 1.8 fusion.10
  103.9 0.0 copy-start
  103.9 2.1 %fusion.11 = f32[8,128,128]{2,1,0:T(8,128)S(1)} fusion(f32[8,128,512]{2,1,0:T(8,128)S(1)} %fusion.10), kind=kOutput, calls=%fused_computation.153 | convolution fusion | flops 805306368 | bytes 2621440 | tf_op jit(solution)/shard_map/mik,mjk->mij/dot_general | solution.py:28
  106.0 11.3 %all_to_all.34 = f32[8,128,128]{2,1,0:T(8,128)S(1)} all-to-all(f32[8,128,128]{2,1,0:T(8,128)S(1)} %fusion.11), channel_id=1, replica_groups=mesh['shard'=64,'model'=4] {'model'}, dimensions={0} | all-to-all | bytes 1048576 | tf_op jit(solution)/shard_map/all_to_all | solution.py:29
  117.4 0.3 fusion.2
  117.6 0.3 fusion.12
  117.9 0.3 fusion.13
  118.2 0.3 fusion.1
  118.5 0.3 fusion.16
  118.7 0.3 fusion.14
  119.0 0.3 fusion.15
  119.3 0.3 fusion
  119.6 0.3 fusion.17
  119.8 12.8 %all_gather.7 = f32[8,128,128]{2,1,0:T(8,128)S(1)} all-gather(f32[2,128,128]{2,1,0:T(8,128)S(1)} %fusion.17), channel_id=1, replica_groups=mesh['shard'=64,'model'=4] {'model'}, dimensions={0}, use_global_device_ids=true | all-gather | bytes 655360 | tf_op jit(solution)/shard_map/all_gather | solution.py:41
  132.6 1.8 fusion.18
  136.2 57.8 %all_to_all.35 = f32[64,8,2,512]{3,2,1,0:T(2,128)S(1)} all-to-all(f32[64,8,2,512]{3,2,1,0:T(2,128)S(1)} %constant_dynamic-update-slice_fusion), channel_id=1, replica_groups=mesh['shard'=64,'model'=4] {'shard'}, dimensions={0} | all-to-all | bytes 4194304 | tf_op jit(solution)/shard_map/all_to_all | solution.py:43
  194.0 3.3 %bitcast_subtract_fusion = f32[512,2,512]{2,1,0:T(2,128)} fusion(f32[64,8,2,512]{3,2,1,0:T(2,128)S(1)} %all_to_all.35, f32[512,2,512]{2,1,0:T(2,128)S(1)} %copy-done.3), kind=kLoop, calls=%fused_computation | loop fusion | flops 1048576 | bytes 6291456 | tf_op jit(solution)/shard_map/sub | solution.py:46
  (75 shorter events, 1.5 us)
Async XLA Ops:
  4.3 63.1 %copy-start.2 = (f32[512,2,512]{2,1,0:T(2,128)}, f32[512,2,512]{2,1,0:T(2,128)S(1)}, u32[]{:S(2)}) copy-start(f32[512,2,512]{2,1,0:T(2,128)S(1)} %multiply_add_fusion) | copy-start | bytes 6291460
  75.0 12.5 %all-to-all-start.1 = ((f32[8,128,128]{2,1,0:T(8,128)}), f32[8,128,128]{2,1,0:T(8,128)S(1)}, u32[]{:S(2)}, u32[]{:S(2)}) async-start(f32[8,128,128]{2,1,0:T(8,128)} %fusion.8), calls=%async_computation.1 | async-start | bytes 1048576 | tf_op jit(solution)/shard_map/all_to_all | solution.py:29
  103.9 2.1 %copy-start = (f32[8,128,512]{2,1,0:T(8,128)}, f32[8,128,512]{2,1,0:T(8,128)S(1)}, u32[]{:S(2)}) copy-start(f32[8,128,512]{2,1,0:T(8,128)S(1)} %fusion.10) | copy-start | bytes 6291460
  117.3 15.3 %copy-start.1 = (f32[8,128,512]{2,1,0:T(8,128)S(1)}, f32[8,128,512]{2,1,0:T(8,128)}, u32[]{:S(2)}) copy-start(f32[8,128,512]{2,1,0:T(8,128)} %copy-done) | copy-start | bytes 6291460
  136.2 57.8 %copy-start.3 = (f32[512,2,512]{2,1,0:T(2,128)S(1)}, f32[512,2,512]{2,1,0:T(2,128)}, u32[]{:S(2)}) copy-start(f32[512,2,512]{2,1,0:T(2,128)} %param.5) | copy-start | bytes 6291460
